TPU v7x, 32 devices: a whole 2x2x4 slice. The times are simulated.
32 devices in a mesh: ulysses: 8 (over z, x), blk: 4 (over y, core).
Axes of the slice: x: 2, y: 2, z: 4, core: 2. Of those that a mesh axis runs over, the one named last changes fastest.
Arguments:
- queries: bfloat16 [4, 512, 4096], P('blk', 'ulysses'), may hold values from -6 to 6
- key_rows: bfloat16 [4, 512, 1024], P('blk', 'ulysses'), may hold values from -6 to 6
- value_rows: bfloat16 [4, 512, 1024], P('blk', 'ulysses'), may hold values from -6 to 6
- tile_segment: int32 [16], replicated, may hold values from 0 to 3, never falling along the last dimension, each value on 1 to 8 neighbouring positions
Outputs:
- attended: bfloat16 [4, 512, 4096], P('blk', 'ulysses')
Inputs may be any that keep to these rules, and one draw needn't show every extreme that they name: `tile_segment`: segment numbers never fall along the sequence and each segment covers 1 to 8 tiles.
All inputs are finite; a program needn't handle non-finite values.
Results may differ from a plain program's by a relative error of at most 0.0045.
Values may be sent and summed in bfloat16 or wider, within the bound.
A program may use at most 64 MiB of HBM per device.

v0:
```python
import math
import jax
import jax.numpy as jnp
from jax import lax
from jax.sharding import PartitionSpec as P

HEAD_DIM = 128
TILE = 128
masked_score = -1e30


def segment_of(positions, tile_segment):
    tiles_total = tile_segment.shape[0]
    matches = (positions // TILE)[:, None] == jnp.arange(tiles_total, dtype=jnp.int32)[None, :]
    return jnp.sum(jnp.where(matches, tile_segment[None, :], 0), axis=1)


def visible(query_pos, query_seg, key_pos, key_seg):
    earlier = key_pos[None, :] <= query_pos[:, None]
    same_image = (key_seg[None, :] == query_seg[:, None]) & (query_seg[:, None] % 2 == 1)
    return earlier | same_image


def widen(source_rows, groups):
    tokens_dev = source_rows.shape[1]
    heads_here = source_rows.shape[2] // HEAD_DIM
    factor = max(1, groups // heads_here)
    spread = jnp.repeat(source_rows.reshape(1, tokens_dev, heads_here, HEAD_DIM), factor, axis=2)
    return spread.reshape(1, tokens_dev, heads_here * factor * HEAD_DIM)


def same_rows(row_ids):
    return row_ids


def update(current, allowed, query_block, key_block, value_block):
    maxima, denominators, weighted = current
    scores = jnp.einsum(
        "qkgd,skd->kgqs", query_block, key_block, preferred_element_type=jnp.float32
    )
    scores = jnp.where(allowed[None, None], scores * HEAD_DIM ** (-0.5), masked_score)
    new_max = jnp.maximum(maxima, jnp.max(scores, axis=3))
    weights = jnp.where(allowed[None, None], jnp.exp(scores - new_max[..., None]), 0.0)
    factor = jnp.exp(maxima - new_max)
    denominators = factor * denominators + jnp.sum(weights, axis=3)
    product = jnp.einsum(
        "kgqs,skd->kgqd",
        weights.astype(jnp.bfloat16),
        value_block,
        preferred_element_type=jnp.float32,
    )
    weighted = factor[..., None] * weighted + product
    return (new_max, denominators, weighted)


def keep_state(current, allowed, query_block, key_block, value_block):
    return current


def build_fold(query_rows, query_pos, tile_segment, key_position, kv_width):
    rows_total = query_rows.shape[0]
    kv_local = kv_width // HEAD_DIM
    group_size = query_rows.shape[1] // HEAD_DIM // kv_local
    shaped = query_rows.reshape(rows_total, kv_local, group_size, HEAD_DIM)
    query_seg = segment_of(query_pos, tile_segment)
    half_rows = rows_total // 2

    def fold_step(running, portion, offset):
        key_part, value_part = portion
        portion_rows = key_part.shape[0]
        block_rows = math.gcd(portion_rows, 512)
        block_total = portion_rows // block_rows
        key_blocks = key_part.reshape(block_total, block_rows, kv_local, HEAD_DIM)
        value_blocks = value_part.reshape(block_total, block_rows, kv_local, HEAD_DIM)

        def one_block(halves, inputs):
            key_block, value_block, block_number = inputs
            key_pos = key_position(
                block_number * block_rows + jnp.arange(block_rows, dtype=jnp.int32)
            )
            key_seg = segment_of(key_pos, tile_segment)
            results = []
            for half_index in range(2):
                row_low = half_index * half_rows
                row_high = row_low + half_rows
                allowed = visible(
                    query_pos[row_low:row_high], query_seg[row_low:row_high], key_pos, key_seg
                )
                results.append(
                    lax.cond(
                        jnp.any(allowed),
                        update,
                        keep_state,
                        halves[half_index],
                        allowed,
                        shaped[row_low:row_high],
                        key_block,
                        value_block,
                    )
                )
            return ((results[0], results[1]), None)

        running, unused = lax.scan(
            one_block, running, (key_blocks, value_blocks, jnp.arange(block_total, dtype=jnp.int32))
        )
        return running

    def empty_half():
        return (
            jnp.full((kv_local, group_size, half_rows), masked_score, jnp.float32),
            jnp.zeros((kv_local, group_size, half_rows), jnp.float32),
            jnp.zeros((kv_local, group_size, half_rows, HEAD_DIM), jnp.float32),
        )

    return (fold_step, (empty_half(), empty_half()))


def finish(running):
    outputs = [weighted / denominators[..., None] for maxima, denominators, weighted in running]
    joined = jnp.concatenate(outputs, axis=2)
    kv_local, group_size, rows_total, head_dim = joined.shape
    joined = jnp.transpose(joined, (2, 0, 1, 3)).reshape(
        rows_total, kv_local * group_size * head_dim
    )
    return joined.astype(jnp.bfloat16)


def local(queries, key_rows, value_rows, tile_segment):
    ulysses_count = lax.axis_size("ulysses")
    tokens_dev = queries.shape[1]
    block_len = tokens_dev * ulysses_count
    block_index = lax.axis_index("blk")
    local_rows = jnp.arange(block_len, dtype=jnp.int32)
    moved = (
        lax.all_to_all(queries, "ulysses", split_axis=2, concat_axis=1, tiled=True),
        lax.all_to_all(
            widen(key_rows, ulysses_count), "ulysses", split_axis=2, concat_axis=1, tiled=True
        ),
        lax.all_to_all(
            widen(value_rows, ulysses_count), "ulysses", split_axis=2, concat_axis=1, tiled=True
        ),
    )
    query_rows, key_local, value_local = (moved[0][0], moved[1][0], moved[2][0])
    query_pos = block_index * block_len + local_rows
    fold_step, initial = build_fold(
        query_rows, query_pos, tile_segment, same_rows, key_local.shape[1]
    )
    running = fold_step(
        initial,
        (
            lax.all_gather(key_local, "blk", axis=0, tiled=True),
            lax.all_gather(value_local, "blk", axis=0, tiled=True),
        ),
        jnp.int32(0),
    )
    attended = lax.all_to_all(
        finish(running)[None], "ulysses", split_axis=1, concat_axis=2, tiled=True
    )
    return attended


def solution(mesh):
    return jax.shard_map(
        local,
        mesh=mesh,
        in_specs=(
            P("blk", "ulysses", None),
            P("blk", "ulysses", None),
            P("blk", "ulysses", None),
            P(),
        ),
        out_specs=P("blk", "ulysses", None),
        check_vma=False,
    )
```

profile of v0, /device:TPU:4, one launch (start us, length us, event | category | flops | bytes accessed | tf_op | source)
XLA Modules:
  0.0 138.4 jit_solution(7677934682182908862)
XLA Ops:
  0.0 1.3 copy.59
  1.3 0.6 broadcast.215
  1.9 2.3 %reduce.4 = bf16[1024,64]{1,0:T(8,128)(2,1)S(1)} reduce(bf16[1024,1,64]{2,1,0:T(2,128)(2,1)S(1)} %bitcast.162, bf16[]{:T(256)} %broadcast.215), dimensions={1}, to_apply=%bitcast.126.reduce_sub_computation | reduce | bytes 262146
  4.2 0.9 reshape.154
  5.1 5.8 %all-to-all-start = ((bf16[8,2,4096]{2,1,0:T(2,128)(2,1)}), bf16[8,2,4096]{2,1,0:T(2,128)(2,1)S(1)}, u32[]{:S(2)}, u32[]{:S(2)}) async-start(bf16[8,2,4096]{2,1,0:T(2,128)(2,1)} %reshape.154), calls=%async_computation | async-start | bytes 262144 | tf_op jit(solution)/shard_map/all_to_all | solution.py:136
  11.3 2.3 %reduce.5 = bf16[1024,64]{1,0:T(8,128)(2,1)S(1)} reduce(bf16[1024,1,64]{2,1,0:T(2,128)(2,1)S(1)} %bitcast.163, bf16[]{:T(256)} %broadcast.215), dimensions={1}, to_apply=%bitcast.128.reduce_sub_computation | reduce | bytes 262146
  13.6 0.9 reshape.156
  14.5 3.7 %all-to-all-done = bf16[8,2,4096]{2,1,0:T(2,128)(2,1)S(1)} async-done(((bf16[8,2,4096]{2,1,0:T(2,128)(2,1)}), bf16[8,2,4096]{2,1,0:T(2,128)(2,1)S(1)}, u32[]{:S(2)}, u32[]{:S(2)}) %all-to-all-start) | async-done | bytes 131104 | tf_op jit(solution)/shard_map/all_to_all | solution.py:136
  18.2 3.4 %all-to-all-start.1 = ((bf16[8,2,4096]{2,1,0:T(2,128)(2,1)}), bf16[8,2,4096]{2,1,0:T(2,128)(2,1)S(1)}, u32[]{:S(2)}, u32[]{:S(2)}) async-start(bf16[8,2,4096]{2,1,0:T(2,128)(2,1)} %reshape.156), calls=%async_computation.1 | async-start | bytes 262144 | tf_op jit(solution)/shard_map/all_to_all | solution.py:139
  21.6 2.8 %copy.65 = bf16[1,64,4096]{1,0,2:T(2,128)(2,1)S(1)} copy(bf16[1,64,4096]{2,1,0:T(8,128)(2,1)S(1)} %copy-done) | data formatting | bytes 1048576 | tf_op args[0]
  24.4 22.5 %reduce.6 = bf16[4096,64]{1,0:T(8,128)(2,1)S(1)} reduce(bf16[4096,1,64]{2,1,0:T(2,128)(2,1)S(1)} %bitcast.152, bf16[]{:T(256)} %broadcast.215), dimensions={1}, to_apply=%bitcast.130.reduce_sub_computation | reduce | bytes 1048578
  46.9 1.5 %reshape.158 = bf16[8,2,16384]{2,1,0:T(2,128)(2,1)} reshape(bf16[4096,64]{1,0:T(8,128)(2,1)S(1)} %reduce.6) | data formatting | bytes 1048576
  48.5 5.9 %all-to-all-start.2 = ((bf16[8,2,16384]{2,1,0:T(2,128)(2,1)}), bf16[8,2,16384]{2,1,0:T(2,128)(2,1)}, u32[]{:S(2)}, u32[]{:S(2)}) async-start(bf16[8,2,16384]{2,1,0:T(2,128)(2,1)} %reshape.158), calls=%async_computation.2 | async-start | bytes 1048576 | tf_op jit(solution)/shard_map/all_to_all | solution.py:135
  55.9 6.7 %all_gather.6 = bf16[2048,128]{1,0:T(8,128)(2,1)S(1)} all-gather(bf16[512,128]{1,0:T(8,128)(2,1)S(1)} %bitcast.169), channel_id=1, replica_groups=mesh['ulysses'=8,'blk'=4] {'blk'}, dimensions={0}, use_global_device_ids=true | all-gather | bytes 655360 | tf_op jit(solution)/shard_map/all_gather | solution.py:151
  62.6 7.3 %all_gather.7 = bf16[2048,128]{1,0:T(8,128)(2,1)S(1)} all-gather(bf16[512,128]{1,0:T(8,128)(2,1)S(1)} %bitcast.170), channel_id=1, replica_groups=mesh['ulysses'=8,'blk'=4] {'blk'}, dimensions={0}, use_global_device_ids=true | all-gather | bytes 655360 | tf_op jit(solution)/shard_map/all_gather | solution.py:152
  69.9 4.1 %reshape.159 = bf16[4096,1,64]{2,1,0:T(2,128)(2,1)S(1)} reshape(bf16[8,2,16384]{2,1,0:T(2,128)(2,1)} %all-to-all-done.2) | data formatting | bytes 1048576
  74.0 3.6 %copy.66 = bf16[1,64,4096]{2,1,0:T(8,128)(2,1)} copy(bf16[1,64,4096]{1,0,2:T(2,128)(2,1)S(1)} %bitcast.151) | data formatting | bytes 1048576 | tf_op jit(solution)/shard_map/all_to_all | solution.py:135
  77.6 1.2 copy.81
  79.4 31.0 %while.23 = (s32[]{:T(128)}, f32[1,4,256]{2,1,0:T(4,128)S(1)}, f32[1,4,256]{2,1,0:T(4,128)S(1)}, f32[1,4,256,128]{3,2,1,0:T(8,128)S(1)}, f32[1,4,256]{2,1,0:T(4,...) while((s32[]{:T(128)}, f32[1,4,256]{2,1,0:T(4,128)S(1)}, ...), condition=%wide.region_13.14_spmd, body=%wide.region_1.13_spmd.sunk | while | flops 552381440 | bytes 17462768 | solution.py:103
  79.4 0.6 dynamic_slice.28
  80.8 1.1 fusion.59
  82.5 1.9 %conditional.5 = ((f32[1,4,256]{2,1,0:T(4,128)S(1)}, f32[1,4,256]{2,1,0:T(4,128)S(1)}, f32[1,4,256,128]{3,2,1,0:T(8,128)S(1)})) conditional(s32[]{:T(128)} %convert_element_type.47, (f32[1,4,256]{2,1,0:T(4,128)S(1)}, f32[1,4,256]{2,1,0:T(4,128)S(1)}, f32[1,4,256,128]{3,2,1,0:T(8,128)S(1)}) %tuple.82, (pred[256,512]{0,1:T(8,128)(4,1)S(1)}, ...), branch_computations={%region_9.9_spmd, %region_10.12_spmd} | conditional | flops 275516416 | bytes 8323104 | solution.py:90
  82.5 0.5 fusion.20
  83.0 0.5 fusion.22
  83.6 0.9 fusion.23
  85.2 2.0 %conditional.4 = ((f32[1,4,256]{2,1,0:T(4,128)S(1)}, f32[1,4,256]{2,1,0:T(4,128)S(1)}, f32[1,4,256,128]{3,2,1,0:T(8,128)S(1)})) conditional(s32[]{:T(128)} %convert_element_type.46, (f32[1,4,256]{2,1,0:T(4,128)S(1)}, f32[1,4,256]{2,1,0:T(4,128)S(1)}, f32[1,4,256,128]{3,2,1,0:T(8,128)S(1)}) %tuple.80, (pred[256,512]{0,1:T(8,128)(4,1)S(1)}, ...), branch_computations={%region_4.4_spmd, %region_5.7_spmd} | conditional | flops 275516416 | bytes 8323104 | solution.py:90
  85.2 0.5 fusion
  85.7 0.5 fusion.2
  86.2 0.9 fusion.3
  87.1 0.6 dynamic_slice.28
  88.5 1.1 fusion.59
  90.3 2.0 %conditional.5 = ((f32[1,4,256]{2,1,0:T(4,128)S(1)}, f32[1,4,256]{2,1,0:T(4,128)S(1)}, f32[1,4,256,128]{3,2,1,0:T(8,128)S(1)})) conditional(s32[]{:T(128)} %convert_element_type.47, (f32[1,4,256]{2,1,0:T(4,128)S(1)}, f32[1,4,256]{2,1,0:T(4,128)S(1)}, f32[1,4,256,128]{3,2,1,0:T(8,128)S(1)}) %tuple.82, (pred[256,512]{0,1:T(8,128)(4,1)S(1)}, ...), branch_computations={%region_9.9_spmd, %region_10.12_spmd} | conditional | flops 275516416 | bytes 8323104 | solution.py:90
  90.3 0.5 fusion.20
  90.8 0.5 fusion.22
  91.3 0.9 fusion.23
  92.9 2.0 %conditional.4 = ((f32[1,4,256]{2,1,0:T(4,128)S(1)}, f32[1,4,256]{2,1,0:T(4,128)S(1)}, f32[1,4,256,128]{3,2,1,0:T(8,128)S(1)})) conditional(s32[]{:T(128)} %convert_element_type.46, (f32[1,4,256]{2,1,0:T(4,128)S(1)}, f32[1,4,256]{2,1,0:T(4,128)S(1)}, f32[1,4,256,128]{3,2,1,0:T(8,128)S(1)}) %tuple.80, (pred[256,512]{0,1:T(8,128)(4,1)S(1)}, ...), branch_computations={%region_4.4_spmd, %region_5.7_spmd} | conditional | flops 275516416 | bytes 8323104 | solution.py:90
  92.9 0.5 fusion
  93.4 0.5 fusion.2
  94.0 0.9 fusion.3
  94.9 0.6 dynamic_slice.28
  96.3 1.1 fusion.59
  98.0 1.9 %conditional.5 = ((f32[1,4,256]{2,1,0:T(4,128)S(1)}, f32[1,4,256]{2,1,0:T(4,128)S(1)}, f32[1,4,256,128]{3,2,1,0:T(8,128)S(1)})) conditional(s32[]{:T(128)} %convert_element_type.47, (f32[1,4,256]{2,1,0:T(4,128)S(1)}, f32[1,4,256]{2,1,0:T(4,128)S(1)}, f32[1,4,256,128]{3,2,1,0:T(8,128)S(1)}) %tuple.82, (pred[256,512]{0,1:T(8,128)(4,1)S(1)}, ...), branch_computations={%region_9.9_spmd, %region_10.12_spmd} | conditional | flops 275516416 | bytes 8323104 | solution.py:90
  98.0 0.5 fusion.20
  98.5 0.5 fusion.22
  99.1 0.9 fusion.23
  100.7 2.0 %conditional.4 = ((f32[1,4,256]{2,1,0:T(4,128)S(1)}, f32[1,4,256]{2,1,0:T(4,128)S(1)}, f32[1,4,256,128]{3,2,1,0:T(8,128)S(1)})) conditional(s32[]{:T(128)} %convert_element_type.46, (f32[1,4,256]{2,1,0:T(4,128)S(1)}, f32[1,4,256]{2,1,0:T(4,128)S(1)}, f32[1,4,256,128]{3,2,1,0:T(8,128)S(1)}) %tuple.80, (pred[256,512]{0,1:T(8,128)(4,1)S(1)}, ...), branch_computations={%region_4.4_spmd, %region_5.7_spmd} | conditional | flops 275516416 | bytes 8323104 | solution.py:90
  100.7 0.5 fusion
  101.2 0.5 fusion.2
  101.7 0.9 fusion.3
  102.7 0.6 dynamic_slice.28
  104.0 1.1 fusion.59
  105.8 2.0 %conditional.5 = ((f32[1,4,256]{2,1,0:T(4,128)S(1)}, f32[1,4,256]{2,1,0:T(4,128)S(1)}, f32[1,4,256,128]{3,2,1,0:T(8,128)S(1)})) conditional(s32[]{:T(128)} %convert_element_type.47, (f32[1,4,256]{2,1,0:T(4,128)S(1)}, f32[1,4,256]{2,1,0:T(4,128)S(1)}, f32[1,4,256,128]{3,2,1,0:T(8,128)S(1)}) %tuple.82, (pred[256,512]{0,1:T(8,128)(4,1)S(1)}, ...), branch_computations={%region_9.9_spmd, %region_10.12_spmd} | conditional | flops 275516416 | bytes 8323104 | solution.py:90
  105.8 0.5 fusion.20
  106.3 0.5 fusion.22
  106.9 0.9 fusion.23
  108.4 2.0 %conditional.4 = ((f32[1,4,256]{2,1,0:T(4,128)S(1)}, f32[1,4,256]{2,1,0:T(4,128)S(1)}, f32[1,4,256,128]{3,2,1,0:T(8,128)S(1)})) conditional(s32[]{:T(128)} %convert_element_type.46, (f32[1,4,256]{2,1,0:T(4,128)S(1)}, f32[1,4,256]{2,1,0:T(4,128)S(1)}, f32[1,4,256,128]{3,2,1,0:T(8,128)S(1)}) %tuple.80, (pred[256,512]{0,1:T(8,128)(4,1)S(1)}, ...), branch_computations={%region_4.4_spmd, %region_5.7_spmd} | conditional | flops 275516416 | bytes 8323104 | solution.py:90
  108.4 0.5 fusion
  109.0 0.5 fusion.2
  109.5 0.9 fusion.3
  111.0 0.9 copy.73
  111.9 3.9 %reduce.7 = bf16[512,512]{1,0:T(8,128)(2,1)S(1)} reduce(bf16[512,1,512]{2,1,0:T(2,128)(2,1)S(1)} %bitcast.154, bf16[]{:T(256)} %broadcast.215), dimensions={1}, to_apply=%bitcast.132.reduce_sub_computation | reduce | bytes 1048578
  116.1 20.8 %all_to_all.63 = bf16[8,2,16384]{2,1,0:T(2,128)(2,1)S(1)} all-to-all(bf16[8,2,16384]{2,1,0:T(2,128)(2,1)S(1)} %reshape.160), channel_id=1, replica_groups=mesh['ulysses'=8,'blk'=4] {'ulysses'}, dimensions={0} | all-to-all | bytes 1048576 | tf_op jit(solution)/shard_map/all_to_all | solution.py:156
  136.9 0.5 reshape.161
  137.6 0.8 copy.78
  (84 shorter events, 4.2 us)
Async XLA Ops:
  0.0 10.9 %copy-start.1 = (bf16[1,64,1024]{2,1,0:T(8,128)(2,1)S(1)}, bf16[1,64,1024]{2,1,0:T(8,128)(2,1)}, u32[]{:S(2)}) copy-start(bf16[1,64,1024]{2,1,0:T(8,128)(2,1)} %param.12) | copy-start | bytes 393220
  0.0 21.6 %copy-start = (bf16[1,64,4096]{2,1,0:T(8,128)(2,1)S(1)}, bf16[1,64,4096]{2,1,0:T(8,128)(2,1)}, u32[]{:S(2)}) copy-start(bf16[1,64,4096]{2,1,0:T(8,128)(2,1)} %param.10) | copy-start | bytes 1572868
  5.1 13.1 %all-to-all-start = ((bf16[8,2,4096]{2,1,0:T(2,128)(2,1)}), bf16[8,2,4096]{2,1,0:T(2,128)(2,1)S(1)}, u32[]{:S(2)}, u32[]{:S(2)}) async-start(bf16[8,2,4096]{2,1,0:T(2,128)(2,1)} %reshape.154), calls=%async_computation | async-start | bytes 262144 | tf_op jit(solution)/shard_map/all_to_all | solution.py:136
  18.2 30.3 %all-to-all-start.1 = ((bf16[8,2,4096]{2,1,0:T(2,128)(2,1)}), bf16[8,2,4096]{2,1,0:T(2,128)(2,1)S(1)}, u32[]{:S(2)}, u32[]{:S(2)}) async-start(bf16[8,2,4096]{2,1,0:T(2,128)(2,1)} %reshape.156), calls=%async_computation.1 | async-start | bytes 262144 | tf_op jit(solution)/shard_map/all_to_all | solution.py:139
  24.4 24.0 %copy-start.2 = (s32[16]{0:T(128)S(1)}, s32[16]{0:T(128)}, u32[]{:S(2)}) copy-start(s32[16]{0:T(128)} %param.13) | copy-start | bytes 196
  48.5 21.3 %all-to-all-start.2 = ((bf16[8,2,16384]{2,1,0:T(2,128)(2,1)}), bf16[8,2,16384]{2,1,0:T(2,128)(2,1)}, u32[]{:S(2)}, u32[]{:S(2)}) async-start(bf16[8,2,16384]{2,1,0:T(2,128)(2,1)} %reshape.158), calls=%async_computation.2 | async-start | bytes 1048576 | tf_op jit(solution)/shard_map/all_to_all | solution.py:135
where the time goes:
time: 139 us; the launch traced here: 138 us
  other arithmetic  40.5 us (29%)
  blocking collectives  34.7 us (25%)
  local copies, waits for them, and re-layouts  24.7 us (18%)
  starting transfers between devices  15.1 us (11%)
  matrix products  10.8 us (8%)
  loops' own time  8.49 us (6%)
  waiting for transfers between devices  3.74 us (3%)
    unnamed x4, other arithmetic  31 us
    all_to_all x1, blocking collectives, local(): lax.all_to_all(finish(running)[None], 'ulysses', split_axis=1, concat_axi...  20.8 us
    unnamed x22, local copies, waits for them, and re-layouts  15.4 us
    another operation x1, loops' own time, fold_step(): lax.scan(one_block, running, (key_blocks, value_blocks, jnp.arange(block_...  8.16 us
    all_gather x1, blocking collectives, local(): lax.all_gather(value_local, 'blk', axis=0, tiled=True)  7.26 us
    dot_general x8, matrix products, update(): jnp.einsum('kgqs,skd->kgqd', weights.astype(jnp.bfloat16), value_block, p...  6.93 us
    all_gather x1, blocking collectives, local(): lax.all_gather(key_local, 'blk', axis=0, tiled=True)  6.68 us
    all_to_all x1, starting transfers between devices, local(): lax.all_to_all(queries, 'ulysses', split_axis=2, concat_axis=1, tiled=True)  5.9 us
  transfers between devices with their start and end apart: 3, of which 1 were waited for; matrix products, arithmetic and copies ran while one was open for 23% of the time, Pallas kernels for 0%

commit v1 on v0

--- a/solution.py
+++ b/solution.py
@@ -7,6 +7,14 @@
 HEAD_DIM = 128
 TILE = 128
 masked_score = -1e30
+
+
+def gather_by_exchange(shard, axis, dim):
+    size = lax.axis_size(axis)
+    repeats = [size if d == dim else 1 for d in range(shard.ndim)]
+    return lax.all_to_all(
+        jnp.tile(shard, repeats), axis, split_axis=dim, concat_axis=dim, tiled=True
+    )
 
 
 def segment_of(positions, tile_segment):
@@ -149,7 +157,7 @@
         initial,
         (
             lax.all_gather(key_local, "blk", axis=0, tiled=True),
-            lax.all_gather(value_local, "blk", axis=0, tiled=True),
+            gather_by_exchange(value_local, "blk", 0),
         ),
         jnp.int32(0),
     )

time: 139 us -> 150 us (1.079)
  waiting for transfers between devices: 3.74 us -> 14.9 us
  blocking collectives: 34.7 us -> 29.3 us
  starting transfers between devices: 15.1 us -> 19 us
    all_to_all x1, waiting for transfers between devices: 0.01 us -> 11.2 us  [local(): lax.all_to_all(queries, 'ulysses', split_axis=2, concat_axis=1, tiled=True)]
    all_gather x1 -> x0, blocking collectives: 7.26 us -> none  [local(): lax.all_gather(value_local, 'blk', axis=0, tiled=True)]
    all_gather x1, blocking collectives: 6.68 us -> 10.9 us  [local(): lax.all_gather(key_local, 'blk', axis=0, tiled=True)]
    all_to_all x0 -> x1, starting transfers between devices: none -> 3.95 us  [gather_by_exchange(): lax.all_to_all(jnp.tile(shard, repeats), axis, split_axis=dim, concat_axi...]
    all_to_all x1, waiting for transfers between devices: 3.74 us -> 0.01 us  [local(): lax.all_to_all(widen(key_rows, ulysses_count), 'ulysses', split_axis=2, c...]
    all_to_all x1, waiting for transfers between devices: 0.01 us -> 3.74 us  [local(): lax.all_to_all(widen(value_rows, ulysses_count), 'ulysses', split_axis=2,...]
    all_to_all x1, starting transfers between devices: 5.81 us -> 3.37 us  [local(): lax.all_to_all(widen(key_rows, ulysses_count), 'ulysses', split_axis=2, c...]
    all_to_all x1, starting transfers between devices: 3.37 us -> 5.81 us  [local(): lax.all_to_all(widen(value_rows, ulysses_count), 'ulysses', split_axis=2,...]
  transfers between devices with their start and end apart: 3 -> 4, of which waited for: 1 -> 2; matrix products, arithmetic and copies ran while one was open for 23% -> 28% of each run, Pallas kernels for 0% -> 0%
where the time goes in v1:
time: 150 us; the launch traced here: 149 us
  other arithmetic  40.5 us (27%)
  blocking collectives  29.3 us (20%)
  local copies, waits for them, and re-layouts  25.7 us (17%)
  starting transfers between devices  19 us (13%)
  waiting for transfers between devices  14.9 us (10%)
  matrix products  10.8 us (7%)
  loops' own time  8.49 us (6%)
    unnamed x4, other arithmetic  31 us
    all_to_all x1, blocking collectives, local(): lax.all_to_all(finish(running)[None], 'ulysses', split_axis=1, concat_axi...  18.5 us
    unnamed x24, local copies, waits for them, and re-layouts  15.4 us
    all_to_all x1, waiting for transfers between devices, local(): lax.all_to_all(queries, 'ulysses', split_axis=2, concat_axis=1, tiled=True)  11.2 us
    all_gather x1, blocking collectives, local(): lax.all_gather(key_local, 'blk', axis=0, tiled=True)  10.9 us
    another operation x1, loops' own time, fold_step(): lax.scan(one_block, running, (key_blocks, value_blocks, jnp.arange(block_...  8.16 us
    dot_general x8, matrix products, update(): jnp.einsum('kgqs,skd->kgqd', weights.astype(jnp.bfloat16), value_block, p...  6.93 us
    all_to_all x1, starting transfers between devices, local(): lax.all_to_all(queries, 'ulysses', split_axis=2, concat_axis=1, tiled=True)  5.9 us
  transfers between devices with their start and end apart: 4, of which 2 were waited for; matrix products, arithmetic and copies ran while one was open for 28% of the time, Pallas kernels for 0%

profile of v1, /device:TPU:4, one launch (start us, length us, event | category | flops | bytes accessed | tf_op | source)
XLA Modules:
  0.0 149.1 jit_solution(11274781889114034909)
XLA Ops:
  0.0 1.3 copy.61
  1.3 0.6 broadcast.217
  1.9 2.3 %reduce.5 = bf16[1024,64]{1,0:T(8,128)(2,1)S(1)} reduce(bf16[1024,1,64]{2,1,0:T(2,128)(2,1)S(1)} %bitcast.160, bf16[]{:T(256)} %broadcast.217), dimensions={1}, to_apply=%bitcast.126.reduce_sub_computation | reduce | bytes 262146
  4.2 0.9 reshape.164
  5.1 5.8 %all-to-all-start.1 = ((bf16[8,2,4096]{2,1,0:T(2,128)(2,1)}), bf16[8,2,4096]{2,1,0:T(2,128)(2,1)S(1)}, u32[]{:S(2)}, u32[]{:S(2)}) async-start(bf16[8,2,4096]{2,1,0:T(2,128)(2,1)} %reshape.164), calls=%async_computation.1 | async-start | bytes 262144 | tf_op jit(solution)/shard_map/all_to_all | solution.py:147
  11.3 2.3 %reduce.4 = bf16[1024,64]{1,0:T(8,128)(2,1)S(1)} reduce(bf16[1024,1,64]{2,1,0:T(2,128)(2,1)S(1)} %bitcast.161, bf16[]{:T(256)} %broadcast.217), dimensions={1}, to_apply=%bitcast.124.reduce_sub_computation | reduce | bytes 262146
  13.6 0.9 reshape.162
  14.5 3.7 %all-to-all-done.1 = bf16[8,2,4096]{2,1,0:T(2,128)(2,1)S(1)} async-done(((bf16[8,2,4096]{2,1,0:T(2,128)(2,1)}), bf16[8,2,4096]{2,1,0:T(2,128)(2,1)S(1)}, u32[]{:S(2)}, u32[]{:S(2)}) %all-to-all-start.1) | async-done | bytes 131104 | tf_op jit(solution)/shard_map/all_to_all | solution.py:147
  18.2 3.4 %all-to-all-start = ((bf16[8,2,4096]{2,1,0:T(2,128)(2,1)}), bf16[8,2,4096]{2,1,0:T(2,128)(2,1)S(1)}, u32[]{:S(2)}, u32[]{:S(2)}) async-start(bf16[8,2,4096]{2,1,0:T(2,128)(2,1)} %reshape.162), calls=%async_computation | async-start | bytes 262144 | tf_op jit(solution)/shard_map/all_to_all | solution.py:144
  21.6 2.8 %copy.64 = bf16[1,64,4096]{1,0,2:T(2,128)(2,1)S(1)} copy(bf16[1,64,4096]{2,1,0:T(8,128)(2,1)S(1)} %copy-done.1) | data formatting | bytes 1048576 | tf_op args[0]
  24.4 22.5 %reduce.6 = bf16[4096,64]{1,0:T(8,128)(2,1)S(1)} reduce(bf16[4096,1,64]{2,1,0:T(2,128)(2,1)S(1)} %bitcast.150, bf16[]{:T(256)} %broadcast.217), dimensions={1}, to_apply=%bitcast.128.reduce_sub_computation | reduce | bytes 1048578
  46.9 1.5 %reshape.166 = bf16[8,2,16384]{2,1,0:T(2,128)(2,1)} reshape(bf16[4096,64]{1,0:T(8,128)(2,1)S(1)} %reduce.6) | data formatting | bytes 1048576
  48.4 5.9 %all-to-all-start.3 = ((bf16[8,2,16384]{2,1,0:T(2,128)(2,1)}), bf16[8,2,16384]{2,1,0:T(2,128)(2,1)S(1)}, u32[]{:S(2)}, u32[]{:S(2)}) async-start(bf16[8,2,16384]{2,1,0:T(2,128)(2,1)} %reshape.166), calls=%async_computation.3 | async-start | bytes 1048576 | tf_op jit(solution)/shard_map/all_to_all | solution.py:143
  55.9 11.2 %all-to-all-done.3 = bf16[8,2,16384]{2,1,0:T(2,128)(2,1)S(1)} async-done(((bf16[8,2,16384]{2,1,0:T(2,128)(2,1)}), bf16[8,2,16384]{2,1,0:T(2,128)(2,1)S(1)}, u32[]{:S(2)}, u32[]{:S(2)}) %all-to-all-start.3) | async-done | bytes 524320 | tf_op jit(solution)/shard_map/all_to_all | solution.py:143
  67.1 0.9 tile.9
  68.1 3.9 %all-to-all-start.2 = ((bf16[4,512,128]{2,1,0:T(8,128)(2,1)}), bf16[4,512,128]{2,1,0:T(8,128)(2,1)S(1)}, u32[]{:S(2)}, u32[]{:S(2)}) async-start(bf16[4,512,128]{2,1,0:T(8,128)(2,1)} %tile.9), calls=%async_computation.2 | async-start | bytes 1048576 | tf_op jit(solution)/shard_map/all_to_all | solution.py:15
  72.0 10.9 %all_gather.3 = bf16[2048,128]{1,0:T(8,128)(2,1)S(1)} all-gather(bf16[512,128]{1,0:T(8,128)(2,1)S(1)} %bitcast.168), channel_id=1, replica_groups=mesh['ulysses'=8,'blk'=4] {'blk'}, dimensions={0}, use_global_device_ids=true | all-gather | bytes 655360 | tf_op jit(solution)/shard_map/all_gather | solution.py:159
  82.9 4.1 %reshape.167 = bf16[4096,1,64]{2,1,0:T(2,128)(2,1)S(1)} reshape(bf16[8,2,16384]{2,1,0:T(2,128)(2,1)} %copy-done) | data formatting | bytes 1048576
  87.0 3.6 %copy.65 = bf16[1,64,4096]{2,1,0:T(8,128)(2,1)} copy(bf16[1,64,4096]{1,0,2:T(2,128)(2,1)S(1)} %bitcast.149) | data formatting | bytes 1048576 | tf_op jit(solution)/shard_map/all_to_all | solution.py:143
  90.6 1.2 copy.79
  92.4 31.0 %while.23 = (s32[]{:T(128)}, f32[1,4,256]{2,1,0:T(4,128)S(1)}, f32[1,4,256]{2,1,0:T(4,128)S(1)}, f32[1,4,256,128]{3,2,1,0:T(8,128)S(1)}, f32[1,4,256]{2,1,0:T(4,...) while((s32[]{:T(128)}, f32[1,4,256]{2,1,0:T(4,128)S(1)}, ...), condition=%wide.region_13.14_spmd, body=%wide.region_1.13_spmd.sunk | while | flops 552381440 | bytes 17462768 | solution.py:111
  92.4 0.6 dynamic_slice.28
  93.8 1.1 fusion.59
  95.6 2.0 %conditional.5 = ((f32[1,4,256]{2,1,0:T(4,128)S(1)}, f32[1,4,256]{2,1,0:T(4,128)S(1)}, f32[1,4,256,128]{3,2,1,0:T(8,128)S(1)})) conditional(s32[]{:T(128)} %convert_element_type.47, (f32[1,4,256]{2,1,0:T(4,128)S(1)}, f32[1,4,256]{2,1,0:T(4,128)S(1)}, f32[1,4,256,128]{3,2,1,0:T(8,128)S(1)}) %tuple.82, (pred[256,512]{0,1:T(8,128)(4,1)S(1)}, ...), branch_computations={%region_9.9_spmd, %region_10.12_spmd} | conditional | flops 275516416 | bytes 8323104 | solution.py:98
  95.6 0.5 fusion.20
  96.1 0.5 fusion.22
  96.6 0.9 fusion.23
  98.2 2.0 %conditional.4 = ((f32[1,4,256]{2,1,0:T(4,128)S(1)}, f32[1,4,256]{2,1,0:T(4,128)S(1)}, f32[1,4,256,128]{3,2,1,0:T(8,128)S(1)})) conditional(s32[]{:T(128)} %convert_element_type.46, (f32[1,4,256]{2,1,0:T(4,128)S(1)}, f32[1,4,256]{2,1,0:T(4,128)S(1)}, f32[1,4,256,128]{3,2,1,0:T(8,128)S(1)}) %tuple.80, (pred[256,512]{0,1:T(8,128)(4,1)S(1)}, ...), branch_computations={%region_4.4_spmd, %region_5.7_spmd} | conditional | flops 275516416 | bytes 8323104 | solution.py:98
  98.2 0.5 fusion
  98.7 0.5 fusion.2
  99.3 0.9 fusion.3
  100.2 0.6 dynamic_slice.28
  101.6 1.1 fusion.59
  103.3 2.0 %conditional.5 = ((f32[1,4,256]{2,1,0:T(4,128)S(1)}, f32[1,4,256]{2,1,0:T(4,128)S(1)}, f32[1,4,256,128]{3,2,1,0:T(8,128)S(1)})) conditional(s32[]{:T(128)} %convert_element_type.47, (f32[1,4,256]{2,1,0:T(4,128)S(1)}, f32[1,4,256]{2,1,0:T(4,128)S(1)}, f32[1,4,256,128]{3,2,1,0:T(8,128)S(1)}) %tuple.82, (pred[256,512]{0,1:T(8,128)(4,1)S(1)}, ...), branch_computations={%region_9.9_spmd, %region_10.12_spmd} | conditional | flops 275516416 | bytes 8323104 | solution.py:98
  103.3 0.5 fusion.20
  103.8 0.5 fusion.22
  104.4 0.9 fusion.23
  106.0 1.9 %conditional.4 = ((f32[1,4,256]{2,1,0:T(4,128)S(1)}, f32[1,4,256]{2,1,0:T(4,128)S(1)}, f32[1,4,256,128]{3,2,1,0:T(8,128)S(1)})) conditional(s32[]{:T(128)} %convert_element_type.46, (f32[1,4,256]{2,1,0:T(4,128)S(1)}, f32[1,4,256]{2,1,0:T(4,128)S(1)}, f32[1,4,256,128]{3,2,1,0:T(8,128)S(1)}) %tuple.80, (pred[256,512]{0,1:T(8,128)(4,1)S(1)}, ...), branch_computations={%region_4.4_spmd, %region_5.7_spmd} | conditional | flops 275516416 | bytes 8323104 | solution.py:98
  106.5 0.5 fusion.2
  107.0 0.9 fusion.3
  108.0 0.6 dynamic_slice.28
  109.3 1.1 fusion.59
  111.1 1.9 %conditional.5 = ((f32[1,4,256]{2,1,0:T(4,128)S(1)}, f32[1,4,256]{2,1,0:T(4,128)S(1)}, f32[1,4,256,128]{3,2,1,0:T(8,128)S(1)})) conditional(s32[]{:T(128)} %convert_element_type.47, (f32[1,4,256]{2,1,0:T(4,128)S(1)}, f32[1,4,256]{2,1,0:T(4,128)S(1)}, f32[1,4,256,128]{3,2,1,0:T(8,128)S(1)}) %tuple.82, (pred[256,512]{0,1:T(8,128)(4,1)S(1)}, ...), branch_computations={%region_9.9_spmd, %region_10.12_spmd} | conditional | flops 275516416 | bytes 8323104 | solution.py:98
  111.6 0.5 fusion.22
  112.2 0.9 fusion.23
  113.7 2.0 %conditional.4 = ((f32[1,4,256]{2,1,0:T(4,128)S(1)}, f32[1,4,256]{2,1,0:T(4,128)S(1)}, f32[1,4,256,128]{3,2,1,0:T(8,128)S(1)})) conditional(s32[]{:T(128)} %convert_element_type.46, (f32[1,4,256]{2,1,0:T(4,128)S(1)}, f32[1,4,256]{2,1,0:T(4,128)S(1)}, f32[1,4,256,128]{3,2,1,0:T(8,128)S(1)}) %tuple.80, (pred[256,512]{0,1:T(8,128)(4,1)S(1)}, ...), branch_computations={%region_4.4_spmd, %region_5.7_spmd} | conditional | flops 275516416 | bytes 8323104 | solution.py:98
  113.7 0.5 fusion
  114.2 0.5 fusion.2
  114.8 0.9 fusion.3
  115.7 0.6 dynamic_slice.28
  117.1 1.1 fusion.59
  118.8 2.0 %conditional.5 = ((f32[1,4,256]{2,1,0:T(4,128)S(1)}, f32[1,4,256]{2,1,0:T(4,128)S(1)}, f32[1,4,256,128]{3,2,1,0:T(8,128)S(1)})) conditional(s32[]{:T(128)} %convert_element_type.47, (f32[1,4,256]{2,1,0:T(4,128)S(1)}, f32[1,4,256]{2,1,0:T(4,128)S(1)}, f32[1,4,256,128]{3,2,1,0:T(8,128)S(1)}) %tuple.82, (pred[256,512]{0,1:T(8,128)(4,1)S(1)}, ...), branch_computations={%region_9.9_spmd, %region_10.12_spmd} | conditional | flops 275516416 | bytes 8323104 | solution.py:98
  118.9 0.5 fusion.20
  119.4 0.5 fusion.22
  119.9 0.9 fusion.23
  121.5 2.0 %conditional.4 = ((f32[1,4,256]{2,1,0:T(4,128)S(1)}, f32[1,4,256]{2,1,0:T(4,128)S(1)}, f32[1,4,256,128]{3,2,1,0:T(8,128)S(1)})) conditional(s32[]{:T(128)} %convert_element_type.46, (f32[1,4,256]{2,1,0:T(4,128)S(1)}, f32[1,4,256]{2,1,0:T(4,128)S(1)}, f32[1,4,256,128]{3,2,1,0:T(8,128)S(1)}) %tuple.80, (pred[256,512]{0,1:T(8,128)(4,1)S(1)}, ...), branch_computations={%region_4.4_spmd, %region_5.7_spmd} | conditional | flops 275516416 | bytes 8323104 | solution.py:98
  121.5 0.5 fusion
  122.0 0.5 fusion.2
  122.6 0.9 fusion.3
  124.0 0.9 copy.71
  124.9 3.9 %reduce.7 = bf16[512,512]{1,0:T(8,128)(2,1)S(1)} reduce(bf16[512,1,512]{2,1,0:T(2,128)(2,1)S(1)} %bitcast.152, bf16[]{:T(256)} %broadcast.217), dimensions={1}, to_apply=%bitcast.130.reduce_sub_computation | reduce | bytes 1048578
  129.2 18.5 %all_to_all.69 = bf16[8,2,16384]{2,1,0:T(2,128)(2,1)S(1)} all-to-all(bf16[8,2,16384]{2,1,0:T(2,128)(2,1)S(1)} %reshape.168), channel_id=1, replica_groups=mesh['ulysses'=8,'blk'=4] {'ulysses'}, dimensions={0} | all-to-all | bytes 1048576 | tf_op jit(solution)/shard_map/all_to_all | solution.py:164
  147.6 0.5 reshape.169
  148.3 0.8 copy.76
  (88 shorter events, 5.2 us)
Async XLA Ops:
  0.0 10.9 %copy-start.2 = (bf16[1,64,1024]{2,1,0:T(8,128)(2,1)S(1)}, bf16[1,64,1024]{2,1,0:T(8,128)(2,1)}, u32[]{:S(2)}) copy-start(bf16[1,64,1024]{2,1,0:T(8,128)(2,1)} %param.11) | copy-start | bytes 393220
  0.0 21.6 %copy-start.1 = (bf16[1,64,4096]{2,1,0:T(8,128)(2,1)S(1)}, bf16[1,64,4096]{2,1,0:T(8,128)(2,1)}, u32[]{:S(2)}) copy-start(bf16[1,64,4096]{2,1,0:T(8,128)(2,1)} %param.10) | copy-start | bytes 1572868
  5.1 13.1 %all-to-all-start.1 = ((bf16[8,2,4096]{2,1,0:T(2,128)(2,1)}), bf16[8,2,4096]{2,1,0:T(2,128)(2,1)S(1)}, u32[]{:S(2)}, u32[]{:S(2)}) async-start(bf16[8,2,4096]{2,1,0:T(2,128)(2,1)} %reshape.164), calls=%async_computation.1 | async-start | bytes 262144 | tf_op jit(solution)/shard_map/all_to_all | solution.py:147
  18.2 30.2 %all-to-all-start = ((bf16[8,2,4096]{2,1,0:T(2,128)(2,1)}), bf16[8,2,4096]{2,1,0:T(2,128)(2,1)S(1)}, u32[]{:S(2)}, u32[]{:S(2)}) async-start(bf16[8,2,4096]{2,1,0:T(2,128)(2,1)} %reshape.162), calls=%async_computation | async-start | bytes 262144 | tf_op jit(solution)/shard_map/all_to_all | solution.py:144
  46.9 7.4 %copy-start.3 = (s32[16]{0:T(128)S(1)}, s32[16]{0:T(128)}, u32[]{:S(2)}) copy-start(s32[16]{0:T(128)} %param.13) | copy-start | bytes 196
  48.4 18.7 %all-to-all-start.3 = ((bf16[8,2,16384]{2,1,0:T(2,128)(2,1)}), bf16[8,2,16384]{2,1,0:T(2,128)(2,1)S(1)}, u32[]{:S(2)}, u32[]{:S(2)}) async-start(bf16[8,2,16384]{2,1,0:T(2,128)(2,1)} %reshape.166), calls=%async_computation.3 | async-start | bytes 1048576 | tf_op jit(solution)/shard_map/all_to_all | solution.py:143
  67.1 1.0 copy-start
  68.1 24.2 %all-to-all-start.2 = ((bf16[4,512,128]{2,1,0:T(8,128)(2,1)}), bf16[4,512,128]{2,1,0:T(8,128)(2,1)S(1)}, u32[]{:S(2)}, u32[]{:S(2)}) async-start(bf16[4,512,128]{2,1,0:T(8,128)(2,1)} %tile.9), calls=%async_computation.2 | async-start | bytes 1048576 | tf_op jit(solution)/shard_map/all_to_all | solution.py:15
